TPU v7x, 32 devices: a whole 2x2x4 slice. The times are simulated.
32 devices in a mesh: dp: 8 (over z, y), mp: 4 (over x, core).
Axes of the slice: x: 2, y: 2, z: 4, core: 2. Of those that a mesh axis runs over, the one named last changes fastest.
Arguments:
- image_tokens: bfloat16 [8, 192, 3072], P('dp'), may hold values from -6 to 6
- text_tokens: bfloat16 [8, 64, 3072], P('dp'), may hold values from -6 to 6
- null_prompt: bfloat16 [64, 3072], replicated, may hold values from -6 to 6
- drop_flags: int32 [8], P('dp'), may hold values 0 or 1
- time_index: int32 [8], P('dp'), may hold values from 0 to 31
- modulation: float32 [32, 3, 3072], replicated, may hold values from -3 to 3
- w_up: bfloat16 [3072, 12288], P('dp', 'mp'), may hold values from -0.109375 to 0.109375
- w_down: bfloat16 [12288, 3072], P('mp', 'dp'), may hold values from -0.0546875 to 0.0546875
- d_output: bfloat16 [8, 256, 3072], P('dp'), may hold values from -6 to 6
Outputs:
- block_out: bfloat16 [8, 256, 3072], P('dp')
- d_tokens: bfloat16 [8, 256, 3072], P('dp')
- grad_up: float32 [3072, 12288], P('dp', 'mp')
- grad_down: float32 [12288, 3072], P('mp', 'dp')
- grad_null: float32 [64, 3072], replicated
All inputs are finite; a program needn't handle non-finite values. No bound on the sum of `drop_flags` on one device may be relied on, other than what follows from the above.
Results may differ from a plain program's by a relative error of at most 0.017.
Values may be sent and summed in bfloat16 or wider, within the bound.
A program may use at most 128 MiB of HBM per device.

v0:
```python
import jax
import jax.numpy as jnp
from jax import lax
from jax.sharding import PartitionSpec as P

EPS = 1e-06


def gelu_tanh(values):
    return jax.nn.gelu(values, approximate=True)


def contract_rows(left, right):
    return lax.dot_general(
        left, right, (((0,), (0,)), ((), ())), preferred_element_type=jnp.float32
    )


def contract_cols(left, right):
    return lax.dot_general(
        left, right, (((1,), (1,)), ((), ())), preferred_element_type=jnp.float32
    )


def shards(
    image_tokens,
    text_tokens,
    null_prompt,
    drop_flags,
    time_index,
    modulation,
    w_up,
    w_down,
    d_output,
):
    dropped = drop_flags == 1
    text_in = jnp.where(dropped[:, None, None], null_prompt[None], text_tokens)
    joined = jnp.concatenate([text_in, image_tokens], axis=1)
    levels = jnp.arange(modulation.shape[0], dtype=jnp.int32)
    indicator_matrix = (time_index[:, None] == levels[None, :]).astype(jnp.float32)
    modulation_vectors = jnp.einsum(
        "yi,imr->ymr", indicator_matrix, modulation, precision=lax.Precision.HIGHEST
    )
    shift_modulation = modulation_vectors[:, 0][:, None]
    scale_mod = modulation_vectors[:, 1][:, None]
    gate_mod = modulation_vectors[:, 2][:, None]
    batch, length, width = joined.shape
    joined32 = joined.astype(jnp.float32)
    centred = joined32 - jnp.mean(joined32, axis=-1, keepdims=True)
    inv_std = lax.rsqrt(jnp.mean(centred * centred, axis=-1, keepdims=True) + EPS)
    normed = centred * inv_std
    mod_in = (normed * (1.0 + scale_mod) + shift_modulation).astype(jnp.bfloat16)
    flat_in = mod_in.reshape(batch * length, width)
    full_up, full_down = (
        lax.all_gather(w_up, "dp", axis=0, tiled=True),
        lax.all_gather(w_down, "dp", axis=1, tiled=True),
    )
    preactivation_rows = jnp.dot(flat_in, full_up, preferred_element_type=jnp.float32)
    hidden = gelu_tanh(preactivation_rows).astype(jnp.bfloat16)
    partial_value = jnp.dot(hidden, full_down, preferred_element_type=jnp.float32)
    branch = (
        lax.psum(partial_value.astype(jnp.bfloat16), "mp")
        .astype(jnp.float32)
        .reshape(batch, length, width)
    )
    block_out = (joined32 + gate_mod * branch).astype(jnp.bfloat16)
    d_out32 = d_output.astype(jnp.float32)
    d_branch = (d_out32 * gate_mod).astype(jnp.bfloat16).reshape(batch * length, width)
    hidden_gradient = contract_cols(d_branch, full_down)
    _, gelu_back = jax.vjp(gelu_tanh, preactivation_rows)
    d_pre = gelu_back(hidden_gradient)[0].astype(jnp.bfloat16)
    d_part = contract_cols(d_pre, full_up)
    d_mod = lax.psum(d_part.astype(jnp.bfloat16), "mp").astype(jnp.float32)
    owned_mod, owned_branch = (
        lax.all_to_all(flat_in, "dp", split_axis=1, concat_axis=0, tiled=True),
        lax.all_to_all(d_branch, "dp", split_axis=1, concat_axis=0, tiled=True),
    )
    grad_up = contract_rows(owned_mod, lax.all_gather(d_pre, "dp", axis=0, tiled=True))
    grad_down_t = contract_rows(owned_branch, lax.all_gather(hidden, "dp", axis=0, tiled=True))
    grad_down = grad_down_t.T
    d_normed = d_mod.reshape(batch, length, width) * (1.0 + scale_mod)
    d_full = d_out32 + inv_std * (
        d_normed
        - jnp.mean(d_normed, axis=-1, keepdims=True)
        - normed * jnp.mean(d_normed * normed, axis=-1, keepdims=True)
    )
    text_len = null_prompt.shape[0]
    null_part = jnp.sum(
        jnp.where(dropped[:, None, None], d_full[:, :text_len], jnp.float32(0.0)), axis=0
    )
    grad_null = lax.psum(null_part.astype(jnp.bfloat16), "dp").astype(jnp.float32)
    return (block_out, d_full.astype(jnp.bfloat16), grad_up, grad_down, grad_null)


def solution(mesh):
    placed = (
        P("dp", None, None),
        P("dp", None, None),
        P(),
        P("dp"),
        P("dp"),
        P(),
        P("dp", "mp"),
        P("mp", "dp"),
        P("dp", None, None),
    )
    return jax.shard_map(
        shards,
        mesh=mesh,
        in_specs=placed,
        out_specs=(P("dp", None, None), P("dp", None, None), P("dp", "mp"), P("mp", "dp"), P()),
        check_vma=False,
    )
```

profile of v0, /device:TPU:0, one launch (start us, length us, event | category | flops | bytes accessed | tf_op | source)
XLA Modules:
  0.0 1318.2 jit_solution(9674357997162976993)
XLA Ops:
  11.7 1.5 fusion.13
  13.2 361.5 %all-gather.5.cloned.1.call-done = bf16[3072,3072]{1,0:T(8,128)(2,1)} async-done(((bf16[384,3072]{1,0:T(8,128)(2,1)}), bf16[3072,3072]{1,0:T(8,128)(2,1)}) %all-gather.5.cloned.1.call-update) | async-done | bytes 18874384 | tf_op jit(solution)/shard_map/all_gather | solution.py:55
  374.7 14.2 %multiply_convert_fusion = (bf16[256,3072]{1,0:T(8,128)(2,1)}, f32[256,3072]{1,0:T(8,128)}) fusion(bf16[3072,3072]{1,0:T(8,128)(2,1)} %all-gather.5.cloned.1.call-done, f32[3072]{0:T(1024)S(1)} %bitcast.82, f32[3072]{0:T(1024)S(1)} %bitcast.79, f32[256]{0:T(256)S(1)} %add_rsqrt_fusion, f32[256]{0:T(256)S(1)} %broadcast_multiply_fusion.2, ...), kind=kOutput, calls=%fused_computation.34 | convolution fusion | flops 4845993984 | bytes 25192448 | tf_op jit(solution)/shard_map/dot_general | solution.py:58
  388.9 349.8 %all-gather.7.cloned.1.call-done = bf16[3072,3072]{1,0:T(8,128)(2,1)} async-done(((bf16[3072,384]{1,0:T(8,128)(2,1)}), bf16[3072,3072]{1,0:T(8,128)(2,1)}) %all-gather.7.cloned.1.call-update) | async-done | bytes 18874384 | tf_op jit(solution)/shard_map/all_gather | solution.py:56
  738.7 12.3 fusion.20
  751.0 10.3 convolution_convert_fusion
  761.3 10.3 convolution_convert_fusion.1
  771.7 68.5 %all-reduce.6.cloned.1.call-done = (bf16[256,3072]{1,0:T(8,128)(2,1)}, bf16[256,3072]{1,0:T(8,128)(2,1)}) async-done(((bf16[256,3072]{1,0:T(8,128)(2,1)}, bf16[256,3072]{1,0:T(8,128)(2,1)}), (bf16[256,3072]{1,0:T(8,128)(2,1)}, bf16[256,3072]{1,0:T(8,128)(2,1)})) %all-reduce.6.cloned.1.call-update) | async-done | bytes 3145744 | tf_op jit(solution)/shard_map/psum | solution.py:62
  840.2 4.4 fusion.21
  844.6 1.6 convert_add_fusion
  846.3 1.1 copy-done.7
  847.4 0.8 fusion.34
  849.7 2.5 add_convert_fusion
  852.3 1.3 copy.18
  853.6 5.5 all-to-all-start
  859.4 1.4 copy.19
  860.8 37.9 %all-to-all-done = bf16[256,8,384]{2,0,1:T(8,128)(2,1)} async-done(((bf16[256,8,384]{2,0,1:T(8,128)(2,1)}), bf16[256,8,384]{2,0,1:T(8,128)(2,1)}, u32[]{:S(2)}, u32[]{:S(2)}) %all-to-all-start) | async-done | bytes 1572896 | tf_op jit(solution)/shard_map/all_to_all | solution.py:75
  898.7 3.8 all-to-all-start.1
  902.4 44.3 %all-reduce.4.cloned.1.call-done = bf16[64,3072]{1,0:T(8,128)(2,1)} async-done(((bf16[64,3072]{1,0:T(8,128)(2,1)}), bf16[64,3072]{1,0:T(8,128)(2,1)}) %all-reduce.4.cloned.1.call-update) | async-done | bytes 393232 | tf_op jit(solution)/shard_map/psum | solution.py:91
  946.7 1.9 convert_element_type.92
  948.7 175.1 %all-gather.9.cloned.1.call-done = bf16[2048,3072]{1,0:T(8,128)(2,1)} async-done(((bf16[256,3072]{1,0:T(8,128)(2,1)}), bf16[2048,3072]{1,0:T(8,128)(2,1)}) %all-gather.9.cloned.1.call-update) | async-done | bytes 12582928 | tf_op jit(solution)/shard_map/all_gather | solution.py:78
  1123.7 9.9 fusion.43
  1133.7 166.4 %all-gather.11.cloned.1.call-done = bf16[2048,3072]{1,0:T(8,128)(2,1)} async-done(((bf16[256,3072]{1,0:T(8,128)(2,1)}), bf16[2048,3072]{1,0:T(8,128)(2,1)}) %all-gather.11.cloned.1.call-update) | async-done | bytes 12582928 | tf_op jit(solution)/shard_map/all_gather | solution.py:79
  1300.1 11.2 fusion.44
  (46 shorter events, 4.8 us)
Async XLA Ops:
  7.2 4.0 copy-start
  7.2 3.0 copy-start.8
  7.2 3.0 copy-start.9
  7.2 3.0 copy-start.2
  7.2 367.5 %all-gather.5.cloned.1.call-start = ((), (), s32[]{:S(2)}) async-start(), calls=%async_computation.2 | async-start | bytes 21233664 | tf_op jit(solution)/shard_map/all_gather | solution.py:55
  7.9 730.7 %all-gather.7.cloned.1.call-start = ((), (), s32[]{:S(2)}) async-start(), calls=%async_computation.3 | async-start | bytes 21233664 | tf_op jit(solution)/shard_map/all_gather | solution.py:56
  8.7 831.5 %all-reduce.6.cloned.1.call-start = ((), (), s32[]{:S(2)}) async-start(), calls=%async_computation.7 | async-start | bytes 6291456 | tf_op jit(solution)/shard_map/psum | solution.py:62
  8.7 3.0 copy-start.4
  771.6 175.1 %all-reduce.4.cloned.1.call-start = ((), (), s32[]{:S(2)}) async-start(), calls=%async_computation.6 | async-start | bytes 786432 | tf_op jit(solution)/shard_map/psum | solution.py:91
  840.2 4.4 copy-start.5
  840.2 4.4 copy-start.6
  846.3 1.1 copy-start.7
  848.2 275.5 %all-gather.9.cloned.1.call-start = ((), (), s32[]{:S(2)}) async-start(), calls=%async_computation.4 | async-start | bytes 14155776 | tf_op jit(solution)/shard_map/all_gather | solution.py:78
  848.8 451.3 %all-gather.11.cloned.1.call-start = ((), (), s32[]{:S(2)}) async-start(), calls=%async_computation.5 | async-start | bytes 14155776 | tf_op jit(solution)/shard_map/all_gather | solution.py:79
  852.3 6.9 copy-start.3
  853.6 45.0 %all-to-all-start = ((bf16[256,8,384]{2,0,1:T(8,128)(2,1)}), bf16[256,8,384]{2,0,1:T(8,128)(2,1)}, u32[]{:S(2)}, u32[]{:S(2)}) async-start(bf16[256,8,384]{2,0,1:T(8,128)(2,1)} %copy.18), calls=%async_computation | async-start | bytes 3145728 | tf_op jit(solution)/shard_map/all_to_all | solution.py:75
  898.7 235.0 %all-to-all-start.1 = ((bf16[256,8,384]{2,0,1:T(8,128)(2,1)}), bf16[256,8,384]{2,0,1:T(8,128)(2,1)S(1)}, u32[]{:S(2)}, u32[]{:S(2)}) async-start(bf16[256,8,384]{2,0,1:T(8,128)(2,1)} %copy.19), calls=%async_computation.1 | async-start | bytes 3145728 | tf_op jit(solution)/shard_map/all_to_all | solution.py:76
  1300.1 11.2 copy-start.1
Sparse Core Ops, SparseCore 0:
  9.6 365.1 all-gather.4
  376.3 362.3 all-gather.6
  771.7 68.4 all-reduce.5
  848.4 98.3 all-reduce.3
  948.8 174.9 all-gather.8
  1125.8 174.2 all-gather.10
where the time goes:
time: 1320 us
  waiting for transfers between devices  1210 us (92%)
  matrix products  68.8 us (5%)
  between operations  15.7 us (1%)
  other arithmetic  13.8 us (1%)
    all_gather x1, waiting for transfers between devices, shards(): lax.all_gather(w_up, 'dp', axis=0, tiled=True)  362 us
    all_gather x1, waiting for transfers between devices, shards(): lax.all_gather(w_down, 'dp', axis=1, tiled=True)  350 us
    all_gather x1, waiting for transfers between devices, shards(): lax.all_gather(d_pre, 'dp', axis=0, tiled=True)  175 us
    all_gather x1, waiting for transfers between devices, shards(): lax.all_gather(hidden, 'dp', axis=0, tiled=True)  166 us
    psum x1, waiting for transfers between devices, shards(): lax.psum(partial_value.astype(jnp.bfloat16), 'mp').astype(jnp.float32)  68.5 us
    psum x1, waiting for transfers between devices, shards(): lax.psum(null_part.astype(jnp.bfloat16), 'dp').astype(jnp.float32)  44.3 us
    all_to_all x1, waiting for transfers between devices, shards(): lax.all_to_all(flat_in, 'dp', split_axis=1, concat_axis=0, tiled=True)  37.9 us
  transfers between devices with their start and end apart: 8, of which 7 were waited for; matrix products, arithmetic and copies ran while one was open for 3% of the time, Pallas kernels for 0%

commit v1 on v0

v1 whole, which is shorter than its diff:
```python
import functools

import jax
import jax.numpy as jnp
from jax import lax
from jax.sharding import PartitionSpec as P

EPS = 1e-06
BF16 = jnp.bfloat16
F32 = jnp.float32


def gelu_tanh(values):
    return jax.nn.gelu(values, approximate=True)


def dot(left, right, dims):
    return lax.dot_general(left, right, (dims, ((), ())), preferred_element_type=F32)


def swap(values, axis, size, bit):
    return lax.ppermute(values, axis, [(i, i ^ bit) for i in range(size)])


def shards(
    dp,
    mp,
    image_tokens,
    text_tokens,
    null_prompt,
    drop_flags,
    time_index,
    modulation,
    w_up,
    w_down,
    d_output,
):
    lines = [list(range(parity, dp, 2)) for parity in range(2)]
    per_line = dp // 2
    bits = []
    bit = 1
    while bit < mp:
        bits.append(bit)
        bit *= 2

    d_rows, ff_m = w_up.shape
    f = ff_m // dp
    width = d_rows * dp

    up_own = lax.all_to_all(
        w_up.reshape(d_rows, dp, f).transpose(1, 0, 2), "dp", 0, 0, tiled=True
    ).reshape(width, f)
    down_own = (
        lax.all_to_all(w_down.reshape(dp, f, d_rows), "dp", 0, 0, tiled=True)
        .transpose(1, 0, 2)
        .reshape(f, width)
    )
    up_other = swap(up_own, "dp", dp, 1)
    down_other = swap(down_own, "dp", dp, 1)

    m = lax.axis_index("mp")
    n_text = text_tokens.shape[1] // mp
    n_image = image_tokens.shape[1] // mp
    all_text = text_tokens.shape[1]

    def share(text_part, image_part):
        t = lax.dynamic_slice_in_dim(text_part, m * n_text, n_text, 0)
        i = lax.dynamic_slice_in_dim(image_part, m * n_image, n_image, 0)
        return jnp.concatenate([t, i], axis=0)

    dropped = drop_flags[0] == 1
    joined32 = share(
        jnp.where(dropped, null_prompt, text_tokens[0]), image_tokens[0]
    ).astype(F32)
    d_out32 = share(d_output[0, :all_text], d_output[0, all_text:]).astype(F32)
    level = lax.dynamic_index_in_dim(modulation, time_index[0], 0, keepdims=False)
    shift, scale, gate = level[0][None], level[1][None], level[2][None]
    centred = joined32 - jnp.mean(joined32, axis=-1, keepdims=True)
    inv_std = lax.rsqrt(jnp.mean(centred * centred, axis=-1, keepdims=True) + EPS)
    normed = centred * inv_std
    mod_in = (normed * (1.0 + scale) + shift).astype(BF16)
    d_branch = (d_out32 * gate).astype(BF16)

    def gather(rows):
        rows = lax.all_gather(rows, "dp", axis=0, tiled=True, axis_index_groups=lines)
        for b in reversed(bits):
            rows = jnp.concatenate([rows, swap(rows, "mp", mp, b)], axis=0)
        return rows

    def scatter(own, other, block_own, block_other, contract):
        def product(rows):
            return dot(own[rows], block_own, contract) + dot(other[rows], block_other, contract)

        half = own.shape[0] // 2
        sent = swap(product(slice(half, None)).astype(BF16), "mp", mp, bits[0])
        total = product(slice(0, half)) + sent.astype(F32)
        for b in bits[1:]:
            half = total.shape[0] // 2
            total = total[:half] + swap(total[half:].astype(BF16), "mp", mp, b).astype(F32)
        parts = lax.all_to_all(
            total.astype(BF16).reshape(per_line, -1, width),
            "dp",
            0,
            0,
            tiled=True,
            axis_index_groups=lines,
        )
        return jnp.sum(parts.astype(F32), axis=0)

    tokens = gather(mod_in)
    d_tok = gather(d_branch)

    def half_block(up, down):
        pre = dot(tokens, up, ((1,), (0,)))
        hid, back = jax.vjp(gelu_tanh, pre)
        d_hid = dot(d_tok, down, ((1,), (1,)))
        return hid.astype(BF16), back(d_hid)[0].astype(BF16)

    hid_own, dpre_own = half_block(up_own, down_own)
    hid_other, dpre_other = half_block(up_other, down_other)
    branch = scatter(hid_own, hid_other, down_own, down_other, ((1,), (0,)))
    d_mod = scatter(dpre_own, dpre_other, up_own, up_other, ((1,), (1,)))

    up_sent = dot(tokens, dpre_other, ((0,), (0,))).astype(BF16)
    down_sent = dot(hid_other, d_tok, ((0,), (0,))).astype(BF16)
    up_back = swap(up_sent, "dp", dp, 1)
    down_back = swap(down_sent, "dp", dp, 1)
    g_up = dot(tokens, dpre_own, ((0,), (0,))) + up_back.astype(F32)
    g_down = dot(hid_own, d_tok, ((0,), (0,))) + down_back.astype(F32)
    grad_up = (
        lax.all_to_all(g_up.astype(BF16).reshape(dp, d_rows, f), "dp", 0, 0, tiled=True)
        .transpose(1, 0, 2)
        .reshape(d_rows, ff_m)
        .astype(F32)
    )
    grad_down = (
        lax.all_to_all(
            g_down.astype(BF16).reshape(f, dp, d_rows).transpose(1, 0, 2),
            "dp",
            0,
            0,
            tiled=True,
        )
        .reshape(ff_m, d_rows)
        .astype(F32)
    )

    block_out = (joined32 + gate * branch).astype(BF16)
    d_normed = d_mod * (1.0 + scale)
    d_full = d_out32 + inv_std * (
        d_normed
        - jnp.mean(d_normed, axis=-1, keepdims=True)
        - normed * jnp.mean(d_normed * normed, axis=-1, keepdims=True)
    )
    null_part = jnp.where(dropped, d_full[:n_text], F32(0.0)).astype(BF16)
    null_sum = lax.psum(null_part, "dp")

    def whole(rows):
        every = lax.all_gather(rows, "mp", axis=0)
        return jnp.concatenate(
            [
                every[:, :n_text].reshape(-1, width),
                every[:, n_text:].reshape(-1, width),
            ],
            axis=0,
        )[None]

    grad_null = lax.all_gather(null_sum, "mp", axis=0, tiled=True).astype(F32)
    return (whole(block_out), whole(d_full.astype(BF16)), grad_up, grad_down, grad_null)


def solution(mesh):
    placed = (
        P("dp", None, None),
        P("dp", None, None),
        P(),
        P("dp"),
        P("dp"),
        P(),
        P("dp", "mp"),
        P("mp", "dp"),
        P("dp", None, None),
    )
    return jax.shard_map(
        functools.partial(shards, mesh.shape["dp"], mesh.shape["mp"]),
        mesh=mesh,
        in_specs=placed,
        out_specs=(P("dp", None, None), P("dp", None, None), P("dp", "mp"), P("mp", "dp"), P()),
        check_vma=False,
    )
```

time: 1320 us -> 638 us (0.48)
  waiting for transfers between devices: 1210 us -> 388 us
  local copies, waits for them, and re-layouts: 4.46 us -> 49 us
  other arithmetic: 13.8 us -> 49.7 us
  starting transfers between devices: 9.54 us -> 43.9 us
    all_gather x4, waiting for transfers between devices: 1050 us -> 136 us  [the longest x2 104 us: gather(): lax.all_gather(rows, 'dp', axis=0, tiled=True, axis_index_groups=lines)]
    ppermute x0 -> x12, waiting for transfers between devices: none -> 159 us  [swap(): return lax.ppermute(values, axis, [(i, i ^ bit) for i in range(size)])]
    psum x2 -> x1, waiting for transfers between devices: 113 us -> 25.2 us  [shards(): null_sum = lax.psum(null_part, 'dp')]
    all_to_all x2 -> x6, waiting for transfers between devices: 37.9 us -> 67.6 us  [the longest x1 46 us: shards(): lax.all_to_all(g_down.astype(BF16).reshape(f, dp, d_rows).transpose(1, 0,...]
    all_to_all x2 -> x6, starting transfers between devices: 9.3 us -> 31 us  [the longest x2 8.79 us: scatter(): lax.all_to_all(total.astype(BF16).reshape(per_line, -1, width), 'dp', 0,...]
    unnamed x23 -> x69, local copies, waits for them, and re-layouts: 1.74 us -> 17.3 us
    add x2, other arithmetic: 1.68 us -> 14.9 us  [scatter(): total = product(slice(0, half)) + sent.astype(F32)]
    dot_general x7 -> x16, matrix products: 68.8 us -> 73.8 us  [dot(): lax.dot_general(left, right, (dims, ((), ())), preferred_element_type=F32)]
  transfers between devices with their start and end apart: 8 -> 23, of which waited for: 7 -> 16; matrix products, arithmetic and copies ran while one was open for 3% -> 24% of each run, Pallas kernels for 0% -> 0%
where the time goes in v1:
time: 638 us; the launch traced here: 627 us
  waiting for transfers between devices  388 us (61%)
  matrix products  73.8 us (12%)
  other arithmetic  49.7 us (8%)
  local copies, waits for them, and re-layouts  49 us (8%)
  starting transfers between devices  43.9 us (7%)
  between operations  16.1 us (3%)
  blocking collectives  6.63 us (1%)
    ppermute x12, waiting for transfers between devices, swap(): return lax.ppermute(values, axis, [(i, i ^ bit) for i in range(size)])  159 us
    all_gather x2, waiting for transfers between devices, gather(): lax.all_gather(rows, 'dp', axis=0, tiled=True, axis_index_groups=lines)  104 us
    dot_general x16, matrix products, dot(): lax.dot_general(left, right, (dims, ((), ())), preferred_element_type=F32)  73.8 us
    all_to_all x1, waiting for transfers between devices, shards(): lax.all_to_all(g_down.astype(BF16).reshape(f, dp, d_rows).transpose(1, 0,...  46 us
    all_gather x2, waiting for transfers between devices, whole(): every = lax.all_gather(rows, 'mp', axis=0)  32.1 us
    psum x1, waiting for transfers between devices, shards(): null_sum = lax.psum(null_part, 'dp')  25.2 us
    unnamed x69, local copies, waits for them, and re-layouts  17.3 us
    add x2, other arithmetic, scatter(): total = product(slice(0, half)) + sent.astype(F32)  14.9 us
  transfers between devices with their start and end apart: 23, of which 16 were waited for; matrix products, arithmetic and copies ran while one was open for 24% of the time, Pallas kernels for 0%

profile of v1, /device:TPU:0, one launch (start us, length us, event | category | flops | bytes accessed | tf_op | source)
XLA Modules:
  0.0 627.2 jit_solution(12918581351889117631)
XLA Ops:
  13.5 7.3 %all-to-all-start.1 = ((bf16[8,384,384]{2,1,0:T(8,128)(2,1)}), bf16[8,384,384]{2,1,0:T(8,128)(2,1)S(1)}, u32[]{:S(2)}, u32[]{:S(2)}) async-start(bf16[8,384,384]{2,1,0:T(8,128)(2,1)} %bitcast.115), calls=%async_computation.1 | async-start | bytes 4718592 | tf_op jit(solution)/shard_map/all_to_all | solution.py:54
  22.8 68.6 %all-gather.5.cloned.1.call-done = bf16[256,3072]{1,0:T(8,128)(2,1)} async-done(((bf16[64,3072]{1,0:T(8,128)(2,1)}), bf16[256,3072]{1,0:T(8,128)(2,1)}) %all-gather.5.cloned.1.call-update) | async-done | bytes 1572880 | tf_op jit(solution)/shard_map/all_gather | solution.py:85
  92.9 35.0 %all-gather.9.cloned.1.call-done = bf16[256,3072]{1,0:T(8,128)(2,1)} async-done(((bf16[64,3072]{1,0:T(8,128)(2,1)}), bf16[256,3072]{1,0:T(8,128)(2,1)}) %all-gather.9.cloned.1.call-update) | async-done | bytes 1572880 | tf_op jit(solution)/shard_map/all_gather | solution.py:85
  143.4 20.1 %collective-permute-done.6 = bf16[256,3072]{1,0:T(8,128)(2,1)} collective-permute-done((bf16[256,3072]{1,0:T(8,128)(2,1)}, bf16[256,3072]{1,0:T(8,128)(2,1)}, u32[]{:S(2)}, u32[]{:S(2)}) %collective-permute-start.6) | collective-permute-done | bytes 1572896 | tf_op jit(solution)/shard_map/ppermute | solution.py:22
  180.6 11.9 %all-to-all-done = bf16[8,384,384]{1,2,0:T(8,128)(2,1)} async-done(((bf16[8,384,384]{1,2,0:T(8,128)(2,1)}), bf16[8,384,384]{1,2,0:T(8,128)(2,1)}, u32[]{:S(2)}, u32[]{:S(2)}) %all-to-all-start) | async-done | bytes 2359328 | tf_op jit(solution)/shard_map/all_to_all | solution.py:50
  211.5 17.3 %collective-permute-done.3 = bf16[384,3072]{0,1:T(8,128)(2,1)} collective-permute-done((bf16[384,3072]{0,1:T(8,128)(2,1)S(1)}, bf16[384,3072]{0,1:T(8,128)(2,1)}, u32[]{:S(2)}, u32[]{:S(2)}) %collective-permute-start.3) | collective-permute-done | bytes 2359328 | tf_op jit(solution)/shard_map/ppermute | solution.py:22
  228.8 6.2 fusion.47
  239.4 39.6 %collective-permute-done.2 = bf16[3072,384]{1,0:T(8,128)(2,1)S(1)} collective-permute-done((bf16[3072,384]{1,0:T(8,128)(2,1)}, bf16[3072,384]{1,0:T(8,128)(2,1)S(1)}, u32[]{:S(2)}, u32[]{:S(2)}) %collective-permute-start.2) | collective-permute-done | bytes 2359328 | tf_op jit(solution)/shard_map/ppermute | solution.py:22
  311.6 29.3 %collective-permute-done.10 = bf16[3072,384]{1,0:T(8,128)(2,1)S(1)} collective-permute-done((bf16[3072,384]{1,0:T(8,128)(2,1)S(1)}, bf16[3072,384]{1,0:T(8,128)(2,1)S(1)}, u32[]{:S(2)}, u32[]{:S(2)}) %collective-permute-start.10) | collective-permute-done | bytes 2359328 | tf_op jit(solution)/shard_map/ppermute | solution.py:22
  345.6 6.9 %all-to-all-start.4 = ((bf16[8,384,384]{2,1,0:T(8,128)(2,1)}), bf16[8,384,384]{2,1,0:T(8,128)(2,1)}, u32[]{:S(2)}, u32[]{:S(2)}) async-start(bf16[8,384,384]{2,1,0:T(8,128)(2,1)} %bitcast.116), calls=%async_computation.4 | async-start | bytes 4718592 | tf_op jit(solution)/shard_map/all_to_all | solution.py:131
  352.6 6.3 %fusion.30 = f32[512,3072]{1,0:T(8,128)} fusion(bf16[3072,384]{1,0:T(8,128)(2,1)} %copy-done.2, bf16[1024,384]{1,0:T(8,128)(2,1)S(1)} %copy-done.15), kind=kOutput, calls=%fused_computation.66 | convolution fusion | flops 1207959552 | bytes 9043968 | tf_op jit(solution)/shard_map/dot_general | solution.py:18
  359.0 8.1 %convert_add_fusion = f32[512,3072]{1,0:T(8,128)} fusion(bf16[512,3072]{1,0:T(8,128)(2,1)} %collective-permute-done.8, f32[512,3072]{1,0:T(8,128)S(1)} %bitcast.86, f32[512,3072]{1,0:T(8,128)} %fusion.30), kind=kLoop, calls=%fused_computation | loop fusion | flops 4718592 | bytes 22020096 | tf_op jit(solution)/shard_map/add | solution.py:96
  375.6 6.8 %convert_add_fusion.1 = f32[512,3072]{1,0:T(8,128)} fusion(bf16[512,3072]{1,0:T(8,128)(2,1)} %collective-permute-done.4, f32[512,3072]{1,0:T(8,128)S(1)} %bitcast.84, f32[512,3072]{1,0:T(8,128)S(1)} %fusion.37), kind=kLoop, calls=%fused_computation.2 | loop fusion | flops 4718592 | bytes 22020096 | tf_op jit(solution)/shard_map/add | solution.py:96
  386.3 21.8 %collective-permute-done.9 = bf16[256,3072]{1,0:T(8,128)(2,1)} collective-permute-done((bf16[256,3072]{1,0:T(8,128)(2,1)}, bf16[256,3072]{1,0:T(8,128)(2,1)}, u32[]{:S(2)}, u32[]{:S(2)}) %collective-permute-start.9) | collective-permute-done | bytes 1572896 | tf_op jit(solution)/shard_map/ppermute | solution.py:22
  417.2 7.2 %convolution_convert_fusion = bf16[384,3072]{1,0:T(8,128)(2,1)} fusion(bf16[1024,384]{1,0:T(8,128)(2,1)} %copy-done.13, bf16[1024,3072]{1,0:T(8,128)(2,1)} %constant_dynamic-update-slice_fusion.3), kind=kOutput, calls=%fused_computation.7 | convolution fusion | flops 2417098752 | bytes 9437184 | tf_op jit(solution)/shard_map/dot_general | solution.py:18
  427.8 11.5 %collective-permute-done.5 = bf16[256,3072]{1,0:T(8,128)(2,1)} collective-permute-done((bf16[256,3072]{1,0:T(8,128)(2,1)}, bf16[256,3072]{1,0:T(8,128)(2,1)}, u32[]{:S(2)}, u32[]{:S(2)}) %collective-permute-start.5) | collective-permute-done | bytes 1572896 | tf_op jit(solution)/shard_map/ppermute | solution.py:22
  442.3 6.9 %all-to-all-done.3 = bf16[4,64,3072]{2,1,0:T(8,128)(2,1)} async-done(((bf16[4,64,3072]{2,1,0:T(8,128)(2,1)}), bf16[4,64,3072]{2,1,0:T(8,128)(2,1)}, u32[]{:S(2)}, u32[]{:S(2)}) %all-to-all-start.3) | async-done | bytes 1572896 | tf_op jit(solution)/shard_map/all_to_all | solution.py:100
  453.0 19.4 %collective-permute-done.11 = bf16[384,3072]{1,0:T(8,128)(2,1)} collective-permute-done((bf16[384,3072]{1,0:T(8,128)(2,1)}, bf16[384,3072]{1,0:T(8,128)(2,1)}, u32[]{:S(2)}, u32[]{:S(2)}) %collective-permute-start.11) | collective-permute-done | bytes 2359328 | tf_op jit(solution)/shard_map/ppermute | solution.py:22
  472.4 6.1 add_convert_fusion.2
  501.3 46.0 %all-to-all-done.5 = bf16[8,384,384]{2,1,0:T(8,128)(2,1)S(1)} async-done(((bf16[8,384,384]{2,1,0:T(8,128)(2,1)}), bf16[8,384,384]{2,1,0:T(8,128)(2,1)S(1)}, u32[]{:S(2)}, u32[]{:S(2)}) %all-to-all-start.5) | async-done | bytes 2359328 | tf_op jit(solution)/shard_map/all_to_all | solution.py:137
  550.0 25.2 %all-reduce.2.cloned.1.call-done = bf16[16,3072]{1,0:T(8,128)(2,1)} async-done(((bf16[16,3072]{1,0:T(8,128)(2,1)}), bf16[16,3072]{1,0:T(8,128)(2,1)}) %all-reduce.2.cloned.1.call-update) | async-done | bytes 98320 | tf_op jit(solution)/shard_map/psum | solution.py:156
  575.2 6.6 %all_gather.21 = bf16[64,3072]{1,0:T(8,128)(2,1)S(1)} all-gather(bf16[16,3072]{1,0:T(8,128)(2,1)} %all-reduce.2.cloned.1.call-done), channel_id=1, replica_groups=mesh['dp'=8,'mp'=4] {'mp'}, dimensions={0}, use_global_device_ids=true | all-gather | bytes 491520 | tf_op jit(solution)/shard_map/all_gather | solution.py:168
  582.8 13.1 %all-gather.7.cloned.1.call-done = bf16[4,64,3072]{2,1,0:T(8,128)(2,1)} async-done(((bf16[1,64,3072]{2,1,0:T(8,128)(2,1)}), bf16[4,64,3072]{2,1,0:T(8,128)(2,1)}) %all-gather.7.cloned.1.call-update) | async-done | bytes 1572880 | tf_op jit(solution)/shard_map/all_gather | solution.py:159
  598.6 19.0 %all-gather.11.cloned.1.call-done = bf16[4,64,3072]{2,1,0:T(8,128)(2,1)} async-done(((bf16[1,64,3072]{2,1,0:T(8,128)(2,1)}), bf16[4,64,3072]{2,1,0:T(8,128)(2,1)}) %all-gather.11.cloned.1.call-update) | async-done | bytes 1572880 | tf_op jit(solution)/shard_map/all_gather | solution.py:159
  (166 shorter events, 164.7 us)
Async XLA Ops:
  7.2 84.3 %all-gather.5.cloned.1.call-start = ((), (), s32[]{:S(2)}) async-start(), calls=%async_computation.6 | async-start | bytes 1966080 | tf_op jit(solution)/shard_map/all_gather | solution.py:85
  13.5 120.1 %all-to-all-start.1 = ((bf16[8,384,384]{2,1,0:T(8,128)(2,1)}), bf16[8,384,384]{2,1,0:T(8,128)(2,1)S(1)}, u32[]{:S(2)}, u32[]{:S(2)}) async-start(bf16[8,384,384]{2,1,0:T(8,128)(2,1)} %bitcast.115), calls=%async_computation.1 | async-start | bytes 4718592 | tf_op jit(solution)/shard_map/all_to_all | solution.py:54
  20.9 107.0 %all-gather.9.cloned.1.call-start = ((), (), s32[]{:S(2)}) async-start(), calls=%async_computation.8 | async-start | bytes 1966080 | tf_op jit(solution)/shard_map/all_gather | solution.py:85
  21.9 111.7 %copy-start.12 = (bf16[1,64,3072]{2,1,0:T(8,128)(2,1)}, bf16[1,64,3072]{2,1,0:T(8,128)(2,1)S(1)}, u32[]{:S(2)}) copy-start(bf16[1,64,3072]{2,1,0:T(8,128)(2,1)S(1)} %slice.82) | copy-start | bytes 1179652
  91.4 48.0 %collective-permute-start = (bf16[256,3072]{1,0:T(8,128)(2,1)}, bf16[256,3072]{1,0:T(8,128)(2,1)}, u32[]{:S(2)}, u32[]{:S(2)}) collective-permute-start(bf16[256,3072]{1,0:T(8,128)(2,1)} %all-gather.5.cloned.1.call-done), channel_id=1, source_target_pairs={{0,2},{1,3},{2,0},{3,1},{4,6},{5,7},{6,4},{7,5},{8,10},{9,11},{10,... | collective-permute-start | bytes 4718600 | tf_op jit(solution)/shard_map/ppermute | solution.py:22
  127.9 35.6 %collective-permute-start.6 = (bf16[256,3072]{1,0:T(8,128)(2,1)}, bf16[256,3072]{1,0:T(8,128)(2,1)}, u32[]{:S(2)}, u32[]{:S(2)}) collective-permute-start(bf16[256,3072]{1,0:T(8,128)(2,1)} %all-gather.9.cloned.1.call-done), channel_id=1, source_target_pairs={{0,2},{1,3},{2,0},{3,1},{4,6},{5,7},{6,4},{7,5},{8,10},{9,11},{10,... | collective-permute-start | bytes 4718600 | tf_op jit(solution)/shard_map/ppermute | solution.py:22
  135.1 57.4 %all-to-all-start = ((bf16[8,384,384]{1,2,0:T(8,128)(2,1)}), bf16[8,384,384]{1,2,0:T(8,128)(2,1)}, u32[]{:S(2)}, u32[]{:S(2)}) async-start(bf16[8,384,384]{1,2,0:T(8,128)(2,1)} %bitcast.103), calls=%async_computation | async-start | bytes 4718592 | tf_op jit(solution)/shard_map/all_to_all | solution.py:50
  143.4 54.9 %collective-permute-start.1 = (bf16[512,3072]{1,0:T(8,128)(2,1)}, bf16[512,3072]{1,0:T(8,128)(2,1)}, u32[]{:S(2)}, u32[]{:S(2)}) collective-permute-start(bf16[512,3072]{1,0:T(8,128)(2,1)} %pad_maximum_fusion), channel_id=1, source_target_pairs={{0,1},{1,0},{2,3},{3,2},{4,5},{5,4},{6,7},{7,6},{8,9},{9,8},{10,11... | collective-permute-start | bytes 9437192 | tf_op jit(solution)/shard_map/ppermute | solution.py:22
  166.7 35.3 %collective-permute-start.7 = (bf16[512,3072]{1,0:T(8,128)(2,1)}, bf16[512,3072]{1,0:T(8,128)(2,1)}, u32[]{:S(2)}, u32[]{:S(2)}) collective-permute-start(bf16[512,3072]{1,0:T(8,128)(2,1)} %pad_maximum_fusion.1), channel_id=1, source_target_pairs={{0,1},{1,0},{2,3},{3,2},{4,5},{5,4},{6,7},{7,6},{8,9},{9,8},{10,11... | collective-permute-start | bytes 9437192 | tf_op jit(solution)/shard_map/ppermute | solution.py:22
  171.0 57.8 %collective-permute-start.3 = (bf16[384,3072]{0,1:T(8,128)(2,1)S(1)}, bf16[384,3072]{0,1:T(8,128)(2,1)}, u32[]{:S(2)}, u32[]{:S(2)}) collective-permute-start(bf16[384,3072]{0,1:T(8,128)(2,1)S(1)} %bitcast.87), channel_id=1, source_target_pairs={{0,4},{4,0},{8,12},{12,8},{16,20},{20,16},{24,28},{28,24},{1,5},{5... | collective-permute-start | bytes 7077896 | tf_op jit(solution)/shard_map/ppermute | solution.py:22
  196.8 82.3 %collective-permute-start.2 = (bf16[3072,384]{1,0:T(8,128)(2,1)}, bf16[3072,384]{1,0:T(8,128)(2,1)S(1)}, u32[]{:S(2)}, u32[]{:S(2)}) collective-permute-start(bf16[3072,384]{1,0:T(8,128)(2,1)} %bitcast.91), channel_id=1, source_target_pairs={{0,4},{4,0},{8,12},{12,8},{16,20},{20,16},{24,28},{28,24},{1,5},{5... | collective-permute-start | bytes 7077896 | tf_op jit(solution)/shard_map/ppermute | solution.py:22
  287.3 53.5 %collective-permute-start.10 = (bf16[3072,384]{1,0:T(8,128)(2,1)S(1)}, bf16[3072,384]{1,0:T(8,128)(2,1)S(1)}, u32[]{:S(2)}, u32[]{:S(2)}) collective-permute-start(bf16[3072,384]{1,0:T(8,128)(2,1)S(1)} %convolution_convert_fusion.1), channel_id=1, source_target_pairs={{0,4},{4,0},{8,12},{12,8},{16,20},{20,16},{24,28},{28,24},{1,5},{5... | collective-permute-start | bytes 7077896 | tf_op jit(solution)/shard_map/ppermute | solution.py:22
  295.1 63.8 %collective-permute-start.8 = (bf16[512,3072]{1,0:T(8,128)(2,1)}, bf16[512,3072]{1,0:T(8,128)(2,1)}, u32[]{:S(2)}, u32[]{:S(2)}) collective-permute-start(bf16[512,3072]{1,0:T(8,128)(2,1)} %add_convert_fusion), channel_id=1, source_target_pairs={{0,1},{1,0},{2,3},{3,2},{4,5},{5,4},{6,7},{7,6},{8,9},{9,8},{10,11... | collective-permute-start | bytes 9437192 | tf_op jit(solution)/shard_map/ppermute | solution.py:22
  302.2 73.4 %collective-permute-start.4 = (bf16[512,3072]{1,0:T(8,128)(2,1)}, bf16[512,3072]{1,0:T(8,128)(2,1)}, u32[]{:S(2)}, u32[]{:S(2)}) collective-permute-start(bf16[512,3072]{1,0:T(8,128)(2,1)} %add_convert_fusion.1), channel_id=1, source_target_pairs={{0,1},{1,0},{2,3},{3,2},{4,5},{5,4},{6,7},{7,6},{8,9},{9,8},{10,11... | collective-permute-start | bytes 9437192 | tf_op jit(solution)/shard_map/ppermute | solution.py:22
  345.6 66.4 %all-to-all-start.4 = ((bf16[8,384,384]{2,1,0:T(8,128)(2,1)}), bf16[8,384,384]{2,1,0:T(8,128)(2,1)}, u32[]{:S(2)}, u32[]{:S(2)}) async-start(bf16[8,384,384]{2,1,0:T(8,128)(2,1)} %bitcast.116), calls=%async_computation.4 | async-start | bytes 4718592 | tf_op jit(solution)/shard_map/all_to_all | solution.py:131
  370.5 37.6 %collective-permute-start.9 = (bf16[256,3072]{1,0:T(8,128)(2,1)}, bf16[256,3072]{1,0:T(8,128)(2,1)}, u32[]{:S(2)}, u32[]{:S(2)}) collective-permute-start(bf16[256,3072]{1,0:T(8,128)(2,1)} %slice.154), channel_id=1, source_target_pairs={{0,2},{1,3},{2,0},{3,1},{4,6},{5,7},{6,4},{7,5},{8,10},{9,11},{10,... | collective-permute-start | bytes 4718600 | tf_op jit(solution)/shard_map/ppermute | solution.py:22
  385.7 53.6 %collective-permute-start.5 = (bf16[256,3072]{1,0:T(8,128)(2,1)}, bf16[256,3072]{1,0:T(8,128)(2,1)}, u32[]{:S(2)}, u32[]{:S(2)}) collective-permute-start(bf16[256,3072]{1,0:T(8,128)(2,1)} %slice.155), channel_id=1, source_target_pairs={{0,2},{1,3},{2,0},{3,1},{4,6},{5,7},{6,4},{7,5},{8,10},{9,11},{10,... | collective-permute-start | bytes 4718600 | tf_op jit(solution)/shard_map/ppermute | solution.py:22
  412.0 37.2 %all-to-all-start.3 = ((bf16[4,64,3072]{2,1,0:T(8,128)(2,1)}), bf16[4,64,3072]{2,1,0:T(8,128)(2,1)}, u32[]{:S(2)}, u32[]{:S(2)}) async-start(bf16[4,64,3072]{2,1,0:T(8,128)(2,1)} %bitcast.106), calls=%async_computation.3 | async-start | bytes 3145728 | tf_op jit(solution)/shard_map/all_to_all | solution.py:100
  424.5 48.0 %collective-permute-start.11 = (bf16[384,3072]{1,0:T(8,128)(2,1)}, bf16[384,3072]{1,0:T(8,128)(2,1)}, u32[]{:S(2)}, u32[]{:S(2)}) collective-permute-start(bf16[384,3072]{1,0:T(8,128)(2,1)} %convolution_convert_fusion), channel_id=1, source_target_pairs={{0,4},{4,0},{8,12},{12,8},{16,20},{20,16},{24,28},{28,24},{1,5},{5... | collective-permute-start | bytes 7077896 | tf_op jit(solution)/shard_map/ppermute | solution.py:22
  449.2 38.7 %all-to-all-start.2 = ((bf16[4,64,3072]{2,1,0:T(8,128)(2,1)}), bf16[4,64,3072]{2,1,0:T(8,128)(2,1)S(1)}, u32[]{:S(2)}, u32[]{:S(2)}) async-start(bf16[4,64,3072]{2,1,0:T(8,128)(2,1)} %bitcast.105), calls=%async_computation.2 | async-start | bytes 3145728 | tf_op jit(solution)/shard_map/all_to_all | solution.py:100
  452.7 122.5 %all-reduce.2.cloned.1.call-start = ((), (), s32[]{:S(2)}) async-start(), calls=%async_computation.10 | async-start | bytes 196608 | tf_op jit(solution)/shard_map/psum | solution.py:156
  489.0 58.2 %all-to-all-start.5 = ((bf16[8,384,384]{2,1,0:T(8,128)(2,1)}), bf16[8,384,384]{2,1,0:T(8,128)(2,1)S(1)}, u32[]{:S(2)}, u32[]{:S(2)}) async-start(bf16[8,384,384]{2,1,0:T(8,128)(2,1)} %bitcast.101), calls=%async_computation.5 | async-start | bytes 4718592 | tf_op jit(solution)/shard_map/all_to_all | solution.py:137
  492.7 103.3 %all-gather.7.cloned.1.call-start = ((), (), s32[]{:S(2)}) async-start(), calls=%async_computation.7 | async-start | bytes 1966080 | tf_op jit(solution)/shard_map/all_gather | solution.py:159
  495.9 121.7 %all-gather.11.cloned.1.call-start = ((), (), s32[]{:S(2)}) async-start(), calls=%async_computation.9 | async-start | bytes 1966080 | tf_op jit(solution)/shard_map/all_gather | solution.py:159
  (36 other events, 409.8 us)
Sparse Core Ops, SparseCore 0:
  13.6 77.7 all-gather.4
  93.6 34.2 all-gather.8
  485.2 90.0 all-reduce.1
  577.2 18.6 all-gather.6
  597.9 19.6 all-gather.10
